TPU v7x, 256 devices: a whole 4x4x8 slice. The times are simulated.
256 devices in a mesh: ctx: 32 (over x, z), pb: 2 (over core), ga: 4 (over y).
Axes of the slice: x: 4, y: 4, z: 8, core: 2. Of those that a mesh axis runs over, the one named last changes fastest.
Arguments:
- queries: bfloat16 [8192, 12288], P(('ctx', 'pb'), 'ga'), may hold values from -128 to 128
- stretch_keys: bfloat16 [8192, 768], P(('ctx', 'pb'), 'ga'), may hold values from -16 to 16
- stretch_values: bfloat16 [8192, 512], P(('ctx', 'pb'), 'ga'), may hold values from -6 to 6
- prior_cache_keys: bfloat16 [131072, 768], P('ctx', 'ga'), may hold values from -16 to 16
- cache_values: bfloat16 [131072, 512], P('ctx', 'ga'), may hold values from -6 to 6
- block_lengths: int32 [32, 256], P('ctx'), may hold values from 1 to 32, 4096 in all within a row
- compress_weights: float32 [4, 32], P('ga'), may hold values from 0.1 to 1.9
- selections: int32 [128, 4, 13], P(('ctx', 'pb'), 'ga'), may hold values from 1 to 2045, as said below
- gate_logits: float32 [3, 8192, 64], P(None, ('ctx', 'pb'), 'ga'), may hold values from -6 to 6
Outputs:
- attended: bfloat16 [8192, 8192], P(('ctx', 'pb'), 'ga')
Inputs may be any that keep to these rules, and one draw needn't show every extreme that they name: `block_lengths`: each row belongs to one cache shard and sums to 4096; its largest entry is 32. `selections`: each row lists 13 different blocks, never the first or one of the last two blocks of a cache shard (a shard holds 64 blocks). Over the 2 rows of one device and one group at most 2 listed blocks lie in one cache shard, and for each group one cache shard holds exactly 2 of every device's listed blocks.
All inputs are finite; a program needn't handle non-finite values.
Results may differ from a plain program's by a relative error of at most 0.011.
Values may be sent and summed in bfloat16 or wider, within the bound.
A program may use at most 128 MiB of HBM per device.

v0:
```python
import math
import jax
import jax.numpy as jnp
from jax import lax
from jax.sharding import PartitionSpec as P

SBLK = 64
WINDOW = 512
floor_score = -1e30


def passed_along(value, axis, steps):
    count = lax.axis_size(axis)
    first, last = (max(0, -steps), min(count, count - steps))
    return lax.ppermute(value, axis, [(source, source + steps) for source in range(first, last)])


def compress_rows(cache_rows, value_rows, lengths, branch_weights):
    span = cache_rows.shape[0]
    starts = jnp.cumsum(lengths) - lengths
    positions = jnp.arange(span, dtype=jnp.int32)
    group_member = (positions[None, :] >= starts[:, None]) & (
        positions[None, :] < (starts + lengths)[:, None]
    )
    offsets = jnp.sum(jnp.where(group_member, positions[None, :] - starts[:, None], 0), axis=0)
    lookup = jnp.arange(branch_weights.shape[0], dtype=jnp.int32)
    token_weight = jnp.sum(
        jnp.where(offsets[:, None] == lookup[None, :], branch_weights[None, :], 0.0), axis=1
    )
    spread = 1.0 / jnp.sqrt(lengths.astype(jnp.float32))
    matrix = jnp.where(group_member, token_weight[None, :] * spread[:, None], 0.0).astype(
        jnp.bfloat16
    )
    packed_keys = jnp.dot(matrix, cache_rows, preferred_element_type=jnp.float32).astype(
        jnp.bfloat16
    )
    packed_values = jnp.dot(matrix, value_rows, preferred_element_type=jnp.float32).astype(
        jnp.bfloat16
    )
    return (packed_keys, packed_values)


def wanted_blocks(listed_ids, block_total):
    flat_ids = listed_ids.reshape(-1)
    always_on = jnp.array([0, block_total - 2, block_total - 1], dtype=jnp.int32)
    flat_ids = jnp.concatenate([always_on, flat_ids])
    return flat_ids


def slot_table(flat_ids, per_shard, slot_width):
    owners = flat_ids // per_shard
    position = jnp.arange(flat_ids.shape[0], dtype=jnp.int32)
    before = (owners[None, :] == owners[:, None]) & (position[None, :] < position[:, None])
    rank_count = jnp.sum(before.astype(jnp.int32), axis=1)
    return (owners * slot_width + rank_count, flat_ids % per_shard)


def asked_table(slots, offsets, shards, slot_width):
    places = jnp.arange(shards * slot_width, dtype=jnp.int32)
    matches = slots[:, None] == places[None, :]
    full_table = jnp.sum(jnp.where(matches, offsets[:, None], 0), axis=0)
    return full_table.reshape(shards, slot_width)


def on_device(
    queries,
    stretch_keys,
    stretch_values,
    prior_cache_keys,
    cache_values,
    block_lengths,
    compress_weights,
    selections,
    gate_logits,
):
    query_count = queries.shape[0]
    head_count = gate_logits.shape[2]
    key_width = prior_cache_keys.shape[1]
    value_width = cache_values.shape[1]
    score_scale = 1.0 / math.sqrt(key_width)
    query_rows = queries.reshape(query_count * head_count, key_width)
    row_count = query_rows.shape[0]
    shards = lax.axis_size("ctx")
    packed_keys, packed_values = compress_rows(
        prior_cache_keys, cache_values, block_lengths[0], compress_weights[0]
    )
    start_state = (
        jnp.full((row_count,), floor_score, jnp.float32),
        jnp.zeros((row_count,), jnp.float32),
        jnp.zeros((row_count, value_width), jnp.float32),
    )
    piece_keys = lax.all_gather(packed_keys, "ctx", axis=0, tiled=True)
    piece_values = lax.all_gather(packed_values, "ctx", axis=0, tiled=True)
    length = piece_keys.shape[0]
    stride = math.gcd(length, 1024)
    key_block = piece_keys.reshape(length // stride, stride, key_width)
    value_block = piece_values.reshape(length // stride, stride, value_width)

    def absorb(carry_state, operand):
        row_peak, running_total, blended = carry_state
        some_keys, some_values = operand
        scores = (
            lax.dot_general(
                query_rows, some_keys, (((1,), (1,)), ((), ())), preferred_element_type=jnp.float32
            )
            * score_scale
        )
        new_peak = jnp.maximum(row_peak, jnp.max(scores, axis=1))
        factor = jnp.exp(row_peak - new_peak)
        branch_weights = jnp.exp(scores - new_peak[:, None])
        running_total = running_total * factor + jnp.sum(branch_weights, axis=1)
        blended = blended * factor[:, None] + jnp.dot(
            branch_weights.astype(jnp.bfloat16), some_values, preferred_element_type=jnp.float32
        )
        return ((new_peak, running_total, blended), None)

    row_peak, running_total, blended = lax.scan(absorb, start_state, (key_block, value_block))[0]
    compressed_out = (blended / running_total[:, None]).reshape(
        query_count, head_count, value_width
    )
    listed_ids = selections[:, 0, :]
    query_blocks, listed = listed_ids.shape
    per_shard = prior_cache_keys.shape[0] // SBLK
    block_total = per_shard * shards
    slot_bound = max(2, (query_blocks * listed + shards - 1) // shards)
    key_blocks = prior_cache_keys.reshape(per_shard, SBLK, key_width)
    value_blocks = cache_values.reshape(per_shard, SBLK, value_width)
    slot_width = slot_bound + 2
    slots, offsets = slot_table(wanted_blocks(listed_ids, block_total), per_shard, slot_width)
    asked_here = asked_table(slots, offsets, shards, slot_width)
    asked_for = lax.all_to_all(asked_here, "ctx", split_axis=0, concat_axis=0, tiled=True)
    item_count = asked_for.shape[1]
    flat_asked = asked_for.reshape(-1)
    sent_keys = jnp.take(key_blocks, flat_asked, axis=0).reshape(
        shards, item_count, SBLK, key_width
    )
    sent_values = jnp.take(value_blocks, flat_asked, axis=0).reshape(
        shards, item_count, SBLK, value_width
    )
    got_keys = lax.all_to_all(sent_keys, "ctx", split_axis=0, concat_axis=0, tiled=True)
    got_values = lax.all_to_all(sent_values, "ctx", split_axis=0, concat_axis=0, tiled=True)
    picked_keys = jnp.take(got_keys.reshape(shards * slot_width, SBLK, key_width), slots, axis=0)
    picked_values = jnp.take(
        got_values.reshape(shards * slot_width, SBLK, value_width), slots, axis=0
    )
    fixed_keys = picked_keys[:3]
    fixed_values = picked_values[:3]
    listed_keys = picked_keys[3:]
    listed_values = picked_values[3:]
    selected_keys = jnp.concatenate(
        [
            jnp.broadcast_to(fixed_keys[None], (query_blocks, 3, SBLK, key_width)),
            listed_keys.reshape(query_blocks, listed, SBLK, key_width),
        ],
        axis=1,
    ).reshape(query_blocks, (3 + listed) * SBLK, key_width)
    chosen_values = jnp.concatenate(
        [
            jnp.broadcast_to(fixed_values[None], (query_blocks, 3, SBLK, value_width)),
            listed_values.reshape(query_blocks, listed, SBLK, value_width),
        ],
        axis=1,
    ).reshape(query_blocks, (3 + listed) * SBLK, value_width)
    grouped_rows = queries.reshape(query_blocks, query_count // query_blocks, head_count, key_width)
    scores = (
        jnp.einsum(
            "rjve,rse->rjvs", grouped_rows, selected_keys, preferred_element_type=jnp.float32
        )
        * score_scale
    )
    row_peak = jnp.max(scores, axis=3, keepdims=True)
    branch_weights = jnp.exp(scores - row_peak)
    row_total = jnp.sum(branch_weights, axis=3, keepdims=True)
    selected_out = (
        jnp.einsum(
            "bqhk,bkv->bqhv",
            branch_weights.astype(jnp.bfloat16),
            chosen_values,
            preferred_element_type=jnp.float32,
        )
        / row_total
    )
    selected_out = selected_out.reshape(query_count, head_count, value_width)
    reach_count = max(1, WINDOW // query_count)
    earlier_keys = []
    earlier_values = []
    for distance in range(reach_count, 0, -1):
        moved_keys, moved_values = passed_along(
            (stretch_keys, stretch_values), ("ctx", "pb"), distance
        )
        earlier_keys.append(moved_keys)
        earlier_values.append(moved_values)
    window_rows = jnp.concatenate(earlier_keys + [stretch_keys], axis=0)
    window_values = jnp.concatenate(earlier_values + [stretch_values], axis=0)
    first_query = lax.axis_index(("ctx", "pb")) * query_count
    query_pos = first_query + jnp.arange(query_count, dtype=jnp.int32)
    key_pos = (
        first_query - reach_count * query_count + jnp.arange(window_rows.shape[0], dtype=jnp.int32)
    )
    distance_grid = query_pos[:, None] - key_pos[None, :]
    allowed = (distance_grid >= 0) & (distance_grid < WINDOW) & (key_pos[None, :] >= 0)
    near_scores = (
        jnp.einsum(
            "qhd,kd->qhk",
            queries.reshape(query_count, head_count, key_width),
            window_rows,
            preferred_element_type=jnp.float32,
        )
        * score_scale
    )
    near_scores = jnp.where(allowed[:, None, :], near_scores, floor_score)
    near_peak = jnp.max(near_scores, axis=2, keepdims=True)
    near_weights = jnp.exp(near_scores - near_peak)
    near_total = jnp.sum(near_weights, axis=2, keepdims=True)
    windowed_out = (
        jnp.einsum(
            "qhk,kv->qhv",
            near_weights.astype(jnp.bfloat16),
            window_values,
            preferred_element_type=jnp.float32,
        )
        / near_total
    )
    gate_values = jax.nn.sigmoid(gate_logits)
    attended = (
        gate_values[0][..., None] * compressed_out
        + gate_values[1][..., None] * selected_out
        + gate_values[2][..., None] * windowed_out
    )
    return attended.reshape(query_count, head_count * value_width).astype(jnp.bfloat16)


def solution(mesh):
    placed = (
        P(("ctx", "pb"), "ga"),
        P(("ctx", "pb"), "ga"),
        P(("ctx", "pb"), "ga"),
        P("ctx", "ga"),
        P("ctx", "ga"),
        P("ctx", None),
        P("ga", None),
        P(("ctx", "pb"), "ga", None),
        P(None, ("ctx", "pb"), "ga"),
    )
    return jax.shard_map(
        on_device, mesh=mesh, in_specs=placed, out_specs=P(("ctx", "pb"), "ga"), check_vma=False
    )
```

profile of v0, /device:TPU:24, one launch (start us, length us, event | category | flops | bytes accessed | tf_op | source)
XLA Modules:
  0.0 363.3 jit_solution(14902906855570495999)
XLA Ops:
  17.9 11.3 %all-to-all-start = ((s32[32,1,4]{2,1,0:T(1,128)}), s32[32,1,4]{2,1,0:T(1,128)S(1)}, u32[]{:S(2)}, u32[]{:S(2)}) async-start(s32[32,1,4]{2,1,0:T(1,128)} %bitcast.9), calls=%async_computation | async-start | bytes 32768 | tf_op jit(solution)/shard_map/all_to_all | solution.py:131
  49.8 9.3 %all-to-all-start.2 = ((bf16[32,4,64,128]{3,2,1,0:T(8,128)(2,1)}), bf16[32,4,64,128]{3,2,1,0:T(8,128)(2,1)}, u32[]{:S(2)}, u32[]{:S(2)}) async-start(bf16[32,4,64,128]{3,2,1,0:T(8,128)(2,1)} %broadcast_select_fusion.1), calls=%async_computation.2 | async-start | bytes 4194304 | tf_op jit(solution)/shard_map/all_to_all | solution.py:141
  82.3 30.3 %collective-permute-done.5 = bf16[128,128]{0,1:T(8,128)(2,1)S(1)} collective-permute-done((bf16[128,128]{0,1:T(8,128)(2,1)S(1)}, bf16[128,128]{0,1:T(8,128)(2,1)S(1)}, u32[]{:S(2)}, u32[]{:S(2)}) %collective-permute-start.5) | collective-permute-done | bytes 32800 | tf_op jit(solution)/shard_map/ppermute | solution.py:15
  112.5 6.4 %collective-permute-start.6 = (bf16[128,128]{0,1:T(8,128)(2,1)S(1)}, bf16[128,128]{0,1:T(8,128)(2,1)S(1)}, u32[]{:S(2)}, u32[]{:S(2)}) collective-permute-start(bf16[128,128]{0,1:T(8,128)(2,1)S(1)} %copy.92), channel_id=1, source_target_pairs={{0,8},{4,12},{8,16},{12,20},{16,24},{20,28},{24,32},{28,36},{32,40... | collective-permute-start | bytes 98312 | tf_op jit(solution)/shard_map/ppermute | solution.py:15
  128.1 17.3 %all-to-all-start.1 = ((bf16[32,4,64,192]{3,2,1,0:T(8,128)(2,1)}), bf16[32,4,64,192]{3,2,1,0:T(8,128)(2,1)}, u32[]{:S(2)}, u32[]{:S(2)}) async-start(bf16[32,4,64,192]{3,2,1,0:T(8,128)(2,1)} %broadcast_select_fusion), calls=%async_computation.1 | async-start | bytes 8388608 | tf_op jit(solution)/shard_map/all_to_all | solution.py:140
  148.7 6.0 %copy.102 = bf16[8192,192]{1,0:T(8,128)(2,1)} copy(bf16[8192,192]{0,1:T(8,128)(2,1)} %all-gather.3.cloned.1.call-done) | data formatting | bytes 6291456
  154.6 69.5 %all-gather.5.cloned.1.call-done = bf16[8192,128]{1,0:T(8,128)(2,1)} async-done(((bf16[256,128]{1,0:T(8,128)(2,1)}), bf16[8192,128]{1,0:T(8,128)(2,1)}) %all-gather.5.cloned.1.call-update) | async-done | bytes 2097168 | tf_op jit(solution)/shard_map/all_gather | solution.py:93
  224.1 114.3 %while.15 = (s32[]{:T(128)}, f32[2048]{0:T(1024)S(1)}, f32[2048]{0:T(1024)S(1)}, f32[2048,128]{1,0:T(8,128)S(1)}, bf16[8,1024,192]{2,1,0:T(8,128)(2,1)}, /*index...) while((s32[]{:T(128)}, f32[2048]{0:T(1024)S(1)}, ...), condition=%wide.region_7.8_spmd.clone, body=%wide.region_4.7_spmd.clone.sunk | while | flops 1359751168 | bytes 62522500 | solution.py:117
  224.1 5.5 %multiply_reduce_fusion.2 = (f32[2048]{0:T(1024)S(1)}, f32[1024,2048]{1,0:T(8,128)}) fusion(bf16[2048,192]{1,0:T(8,128)(2,1)S(1)} %get-tuple-element.209, bf16[8,1024,192]{2,1,0:T(8,128)(2,1)} %get-tuple-element.208, s32[]{:T(128)} %get-tuple-element.195), kind=kOutput, calls=%fused_computation.5.clone.1 | convolution fusion | flops 809498624 | bytes 9708032 | tf_op jit(solution)/shard_map/while/body/eval_jaxpr/dot_general | solution.py:103
  229.7 4.9 %fusion.72 = f32[2048]{0:T(1024)S(1)} fusion(f32[1024,2048]{1,0:T(8,128)} %get-tuple-element.183, f32[2048]{0:T(1024)S(1)} %select_maximum_fusion.2), kind=kLoop, calls=%fused_computation.7.clone.1 | loop fusion | flops 6289408 | bytes 8404992 | tf_op jit(solution)/shard_map/while/body/eval_jaxpr/reduce_sum | solution.py:111
  238.4 5.6 %multiply_reduce_fusion.2 = (f32[2048]{0:T(1024)S(1)}, f32[1024,2048]{1,0:T(8,128)}) fusion(bf16[2048,192]{1,0:T(8,128)(2,1)S(1)} %get-tuple-element.209, bf16[8,1024,192]{2,1,0:T(8,128)(2,1)} %get-tuple-element.208, s32[]{:T(128)} %get-tuple-element.195), kind=kOutput, calls=%fused_computation.5.clone.1 | convolution fusion | flops 809498624 | bytes 9708032 | tf_op jit(solution)/shard_map/while/body/eval_jaxpr/dot_general | solution.py:103
  244.0 4.9 %fusion.72 = f32[2048]{0:T(1024)S(1)} fusion(f32[1024,2048]{1,0:T(8,128)} %get-tuple-element.183, f32[2048]{0:T(1024)S(1)} %select_maximum_fusion.2), kind=kLoop, calls=%fused_computation.7.clone.1 | loop fusion | flops 6289408 | bytes 8404992 | tf_op jit(solution)/shard_map/while/body/eval_jaxpr/reduce_sum | solution.py:111
  252.7 5.6 %multiply_reduce_fusion.2 = (f32[2048]{0:T(1024)S(1)}, f32[1024,2048]{1,0:T(8,128)}) fusion(bf16[2048,192]{1,0:T(8,128)(2,1)S(1)} %get-tuple-element.209, bf16[8,1024,192]{2,1,0:T(8,128)(2,1)} %get-tuple-element.208, s32[]{:T(128)} %get-tuple-element.195), kind=kOutput, calls=%fused_computation.5.clone.1 | convolution fusion | flops 809498624 | bytes 9708032 | tf_op jit(solution)/shard_map/while/body/eval_jaxpr/dot_general | solution.py:103
  258.3 4.9 %fusion.72 = f32[2048]{0:T(1024)S(1)} fusion(f32[1024,2048]{1,0:T(8,128)} %get-tuple-element.183, f32[2048]{0:T(1024)S(1)} %select_maximum_fusion.2), kind=kLoop, calls=%fused_computation.7.clone.1 | loop fusion | flops 6289408 | bytes 8404992 | tf_op jit(solution)/shard_map/while/body/eval_jaxpr/reduce_sum | solution.py:111
  267.0 5.6 %multiply_reduce_fusion.2 = (f32[2048]{0:T(1024)S(1)}, f32[1024,2048]{1,0:T(8,128)}) fusion(bf16[2048,192]{1,0:T(8,128)(2,1)S(1)} %get-tuple-element.209, bf16[8,1024,192]{2,1,0:T(8,128)(2,1)} %get-tuple-element.208, s32[]{:T(128)} %get-tuple-element.195), kind=kOutput, calls=%fused_computation.5.clone.1 | convolution fusion | flops 809498624 | bytes 9708032 | tf_op jit(solution)/shard_map/while/body/eval_jaxpr/dot_general | solution.py:103
  272.6 4.9 %fusion.72 = f32[2048]{0:T(1024)S(1)} fusion(f32[1024,2048]{1,0:T(8,128)} %get-tuple-element.183, f32[2048]{0:T(1024)S(1)} %select_maximum_fusion.2), kind=kLoop, calls=%fused_computation.7.clone.1 | loop fusion | flops 6289408 | bytes 8404992 | tf_op jit(solution)/shard_map/while/body/eval_jaxpr/reduce_sum | solution.py:111
  281.3 5.6 %multiply_reduce_fusion.2 = (f32[2048]{0:T(1024)S(1)}, f32[1024,2048]{1,0:T(8,128)}) fusion(bf16[2048,192]{1,0:T(8,128)(2,1)S(1)} %get-tuple-element.209, bf16[8,1024,192]{2,1,0:T(8,128)(2,1)} %get-tuple-element.208, s32[]{:T(128)} %get-tuple-element.195), kind=kOutput, calls=%fused_computation.5.clone.1 | convolution fusion | flops 809498624 | bytes 9708032 | tf_op jit(solution)/shard_map/while/body/eval_jaxpr/dot_general | solution.py:103
  286.8 4.9 %fusion.72 = f32[2048]{0:T(1024)S(1)} fusion(f32[1024,2048]{1,0:T(8,128)} %get-tuple-element.183, f32[2048]{0:T(1024)S(1)} %select_maximum_fusion.2), kind=kLoop, calls=%fused_computation.7.clone.1 | loop fusion | flops 6289408 | bytes 8404992 | tf_op jit(solution)/shard_map/while/body/eval_jaxpr/reduce_sum | solution.py:111
  295.6 5.6 %multiply_reduce_fusion.2 = (f32[2048]{0:T(1024)S(1)}, f32[1024,2048]{1,0:T(8,128)}) fusion(bf16[2048,192]{1,0:T(8,128)(2,1)S(1)} %get-tuple-element.209, bf16[8,1024,192]{2,1,0:T(8,128)(2,1)} %get-tuple-element.208, s32[]{:T(128)} %get-tuple-element.195), kind=kOutput, calls=%fused_computation.5.clone.1 | convolution fusion | flops 809498624 | bytes 9708032 | tf_op jit(solution)/shard_map/while/body/eval_jaxpr/dot_general | solution.py:103
  301.1 4.9 %fusion.72 = f32[2048]{0:T(1024)S(1)} fusion(f32[1024,2048]{1,0:T(8,128)} %get-tuple-element.183, f32[2048]{0:T(1024)S(1)} %select_maximum_fusion.2), kind=kLoop, calls=%fused_computation.7.clone.1 | loop fusion | flops 6289408 | bytes 8404992 | tf_op jit(solution)/shard_map/while/body/eval_jaxpr/reduce_sum | solution.py:111
  309.9 5.6 %multiply_reduce_fusion.2 = (f32[2048]{0:T(1024)S(1)}, f32[1024,2048]{1,0:T(8,128)}) fusion(bf16[2048,192]{1,0:T(8,128)(2,1)S(1)} %get-tuple-element.209, bf16[8,1024,192]{2,1,0:T(8,128)(2,1)} %get-tuple-element.208, s32[]{:T(128)} %get-tuple-element.195), kind=kOutput, calls=%fused_computation.5.clone.1 | convolution fusion | flops 809498624 | bytes 9708032 | tf_op jit(solution)/shard_map/while/body/eval_jaxpr/dot_general | solution.py:103
  315.4 4.9 %fusion.72 = f32[2048]{0:T(1024)S(1)} fusion(f32[1024,2048]{1,0:T(8,128)} %get-tuple-element.183, f32[2048]{0:T(1024)S(1)} %select_maximum_fusion.2), kind=kLoop, calls=%fused_computation.7.clone.1 | loop fusion | flops 6289408 | bytes 8404992 | tf_op jit(solution)/shard_map/while/body/eval_jaxpr/reduce_sum | solution.py:111
  324.2 5.6 %multiply_reduce_fusion.2 = (f32[2048]{0:T(1024)S(1)}, f32[1024,2048]{1,0:T(8,128)}) fusion(bf16[2048,192]{1,0:T(8,128)(2,1)S(1)} %get-tuple-element.209, bf16[8,1024,192]{2,1,0:T(8,128)(2,1)} %get-tuple-element.208, s32[]{:T(128)} %get-tuple-element.195), kind=kOutput, calls=%fused_computation.5.clone.1 | convolution fusion | flops 809498624 | bytes 9708032 | tf_op jit(solution)/shard_map/while/body/eval_jaxpr/dot_general | solution.py:103
  329.7 4.9 %fusion.72 = f32[2048]{0:T(1024)S(1)} fusion(f32[1024,2048]{1,0:T(8,128)} %get-tuple-element.183, f32[2048]{0:T(1024)S(1)} %select_maximum_fusion.2), kind=kLoop, calls=%fused_computation.7.clone.1 | loop fusion | flops 6289408 | bytes 8404992 | tf_op jit(solution)/shard_map/while/body/eval_jaxpr/reduce_sum | solution.py:111
  (188 shorter events, 115.0 us)
Async XLA Ops:
  6.5 40.7 %copy-start = (bf16[4096,128]{1,0:T(8,128)(2,1)S(1)}, bf16[4096,128]{1,0:T(8,128)(2,1)}, u32[]{:S(2)}) copy-start(bf16[4096,128]{1,0:T(8,128)(2,1)} %param.16) | copy-start | bytes 3145732
  6.5 142.1 %all-gather.3.cloned.1.call-start = ((), (), s32[]{:S(2)}) async-start(), calls=%async_computation.3 | async-start | bytes 3244032 | tf_op jit(solution)/shard_map/all_gather | solution.py:92
  11.5 17.7 %copy-start.8 = (bf16[128,192]{0,1:T(8,128)(2,1)S(1)}, bf16[128,192]{0,1:T(8,128)(2,1)}, u32[]{:S(2)}) copy-start(bf16[128,192]{0,1:T(8,128)(2,1)} %param.13) | copy-start | bytes 147460
  11.5 32.0 %copy-start.9 = (bf16[128,128]{1,0:T(8,128)(2,1)S(1)}, bf16[128,128]{1,0:T(8,128)(2,1)}, u32[]{:S(2)}) copy-start(bf16[128,128]{1,0:T(8,128)(2,1)} %param.14) | copy-start | bytes 98308
  17.9 28.3 %all-to-all-start = ((s32[32,1,4]{2,1,0:T(1,128)}), s32[32,1,4]{2,1,0:T(1,128)S(1)}, u32[]{:S(2)}, u32[]{:S(2)}) async-start(s32[32,1,4]{2,1,0:T(1,128)} %bitcast.9), calls=%async_computation | async-start | bytes 32768 | tf_op jit(solution)/shard_map/all_to_all | solution.py:131
  29.2 94.3 %collective-permute-start = (bf16[128,192]{0,1:T(8,128)(2,1)S(1)}, bf16[128,192]{0,1:T(8,128)(2,1)S(1)}, u32[]{:S(2)}, u32[]{:S(2)}) collective-permute-start(bf16[128,192]{0,1:T(8,128)(2,1)S(1)} %copy-done.8), channel_id=1, source_target_pairs={{0,16},{4,20},{8,24},{12,28},{16,32},{20,36},{24,40},{28,44},{32,4... | collective-permute-start | bytes 147464 | tf_op jit(solution)/shard_map/ppermute | solution.py:15
  33.8 89.7 %collective-permute-start.1 = (bf16[128,192]{0,1:T(8,128)(2,1)S(1)}, bf16[128,192]{0,1:T(8,128)(2,1)S(1)}, u32[]{:S(2)}, u32[]{:S(2)}) collective-permute-start(bf16[128,192]{0,1:T(8,128)(2,1)S(1)} %copy-done.8), channel_id=1, source_target_pairs={{0,12},{4,16},{8,20},{12,24},{16,28},{20,32},{24,36},{28,40},{32,4... | collective-permute-start | bytes 147464 | tf_op jit(solution)/shard_map/ppermute | solution.py:15
  35.8 87.7 %collective-permute-start.2 = (bf16[128,192]{0,1:T(8,128)(2,1)S(1)}, bf16[128,192]{0,1:T(8,128)(2,1)S(1)}, u32[]{:S(2)}, u32[]{:S(2)}) collective-permute-start(bf16[128,192]{0,1:T(8,128)(2,1)S(1)} %copy-done.8), channel_id=1, source_target_pairs={{0,8},{4,12},{8,16},{12,20},{16,24},{20,28},{24,32},{28,36},{32,40... | collective-permute-start | bytes 147464 | tf_op jit(solution)/shard_map/ppermute | solution.py:15
  40.4 83.2 %collective-permute-start.3 = (bf16[128,192]{0,1:T(8,128)(2,1)S(1)}, bf16[128,192]{0,1:T(8,128)(2,1)S(1)}, u32[]{:S(2)}, u32[]{:S(2)}) collective-permute-start(bf16[128,192]{0,1:T(8,128)(2,1)S(1)} %copy-done.8), channel_id=1, source_target_pairs={{0,4},{4,8},{8,12},{12,16},{16,20},{20,24},{24,28},{28,32},{32,36}... | collective-permute-start | bytes 147464 | tf_op jit(solution)/shard_map/ppermute | solution.py:15
  43.6 36.1 %collective-permute-start.4 = (bf16[128,128]{0,1:T(8,128)(2,1)S(1)}, bf16[128,128]{0,1:T(8,128)(2,1)S(1)}, u32[]{:S(2)}, u32[]{:S(2)}) collective-permute-start(bf16[128,128]{0,1:T(8,128)(2,1)S(1)} %copy.92), channel_id=1, source_target_pairs={{0,16},{4,20},{8,24},{12,28},{16,32},{20,36},{24,40},{28,44},{32,4... | collective-permute-start | bytes 98312 | tf_op jit(solution)/shard_map/ppermute | solution.py:15
  49.8 78.2 %all-to-all-start.2 = ((bf16[32,4,64,128]{3,2,1,0:T(8,128)(2,1)}), bf16[32,4,64,128]{3,2,1,0:T(8,128)(2,1)}, u32[]{:S(2)}, u32[]{:S(2)}) async-start(bf16[32,4,64,128]{3,2,1,0:T(8,128)(2,1)} %broadcast_select_fusion.1), calls=%async_computation.2 | async-start | bytes 4194304 | tf_op jit(solution)/shard_map/all_to_all | solution.py:141
  59.2 5.9 %copy-start.3 = (bf16[128,3072]{1,0:T(8,128)(2,1)S(1)}, bf16[128,3072]{1,0:T(8,128)(2,1)}, u32[]{:S(2)}) copy-start(bf16[128,3072]{1,0:T(8,128)(2,1)} %param.12) | copy-start | bytes 2359300
  59.2 164.9 %all-gather.5.cloned.1.call-start = ((), (), s32[]{:S(2)}) async-start(), calls=%async_computation.4 | async-start | bytes 2162688 | tf_op jit(solution)/shard_map/all_gather | solution.py:93
  61.1 8.5 %copy-start.18 = (s32[3,1]{0,1:T(1,128)S(1)}, s32[3,1]{0,1:T(1,128)}, u32[]{:S(2)}) copy-start(s32[3,1]{0,1:T(1,128)} %constant.143) | copy-start | bytes 40
  61.1 8.6 %copy-start.10 = (f32[3,128,16]{1,2,0:T(8,128)S(1)}, f32[3,128,16]{1,2,0:T(8,128)}, u32[]{:S(2)}) copy-start(f32[3,128,16]{1,2,0:T(8,128)} %param.20) | copy-start | bytes 73732
  75.1 48.5 %copy-start.6 = (bf16[128,3072]{0,1:T(8,128)(2,1)S(1)}, bf16[128,3072]{0,1:T(8,128)(2,1)}, u32[]{:S(2)}) copy-start(bf16[128,3072]{0,1:T(8,128)(2,1)} %copy.91) | copy-start | bytes 2359300
  79.7 32.8 %collective-permute-start.5 = (bf16[128,128]{0,1:T(8,128)(2,1)S(1)}, bf16[128,128]{0,1:T(8,128)(2,1)S(1)}, u32[]{:S(2)}, u32[]{:S(2)}) collective-permute-start(bf16[128,128]{0,1:T(8,128)(2,1)S(1)} %copy.92), channel_id=1, source_target_pairs={{0,12},{4,16},{8,20},{12,24},{16,28},{20,32},{24,36},{28,40},{32,4... | collective-permute-start | bytes 98312 | tf_op jit(solution)/shard_map/ppermute | solution.py:15
  112.5 8.1 %collective-permute-start.6 = (bf16[128,128]{0,1:T(8,128)(2,1)S(1)}, bf16[128,128]{0,1:T(8,128)(2,1)S(1)}, u32[]{:S(2)}, u32[]{:S(2)}) collective-permute-start(bf16[128,128]{0,1:T(8,128)(2,1)S(1)} %copy.92), channel_id=1, source_target_pairs={{0,8},{4,12},{8,16},{12,20},{16,24},{20,28},{24,32},{28,36},{32,40... | collective-permute-start | bytes 98312 | tf_op jit(solution)/shard_map/ppermute | solution.py:15
  120.7 2.1 collective-permute-start.7
  128.1 19.6 %copy-start.16 = (pred[29]{0:T(512)(128)(4,1)S(1)}, pred[29]{0:T(512)(128)(4,1)}, u32[]{:S(2)}) copy-start(pred[29]{0:T(512)(128)(4,1)} %get-tuple-element.122) | copy-start | bytes 91
  128.1 211.2 %all-to-all-start.1 = ((bf16[32,4,64,192]{3,2,1,0:T(8,128)(2,1)}), bf16[32,4,64,192]{3,2,1,0:T(8,128)(2,1)}, u32[]{:S(2)}, u32[]{:S(2)}) async-start(bf16[32,4,64,192]{3,2,1,0:T(8,128)(2,1)} %broadcast_select_fusion), calls=%async_computation.1 | async-start | bytes 8388608 | tf_op jit(solution)/shard_map/all_to_all | solution.py:140
  229.7 5.8 %copy-start.2 = (f32[1024,2048]{1,0:T(8,128)S(1)}, f32[1024,2048]{1,0:T(8,128)}, u32[]{:S(2)}) copy-start(f32[1024,2048]{1,0:T(8,128)} %get-tuple-element.183) | copy-start | bytes 25165828 | tf_op jit(solution)/shard_map/while
  258.3 5.8 %copy-start.2 = (f32[1024,2048]{1,0:T(8,128)S(1)}, f32[1024,2048]{1,0:T(8,128)}, u32[]{:S(2)}) copy-start(f32[1024,2048]{1,0:T(8,128)} %get-tuple-element.183) | copy-start | bytes 25165828 | tf_op jit(solution)/shard_map/while
  349.5 7.0 %copy-start.1 = (bf16[4096,128]{1,0:T(8,128)(2,1)S(1)}, bf16[4096,128]{1,0:T(8,128)(2,1)}, u32[]{:S(2)}) copy-start(bf16[4096,128]{1,0:T(8,128)(2,1)} %param.16) | copy-start | bytes 3145732
  (16 other events, 57.5 us)
Sparse Core Ops, SparseCore 0:
  15.0 112.5 all-gather.2
  130.1 93.9 all-gather.4
where the time goes:
time: 365 us; the launch traced here: 363 us
  waiting for transfers between devices  102 us (28%)
  matrix products  82.9 us (23%)
  starting transfers between devices  65.1 us (18%)
  other arithmetic  57.9 us (16%)
  local copies, waits for them, and re-layouts  40.9 us (11%)
  between operations  14.1 us (4%)
    all_gather x1, waiting for transfers between devices, on_device(): piece_values = lax.all_gather(packed_values, 'ctx', axis=0, tiled=True)  69.5 us
    dot_general x8, matrix products, absorb(): lax.dot_general(query_rows, some_keys, (((1,), (1,)), ((), ())), preferre...  44.4 us
    reduce_sum x8, other arithmetic, absorb(): running_total = running_total * factor + jnp.sum(branch_weights, axis=1)  39.5 us
    ppermute x8, waiting for transfers between devices, passed_along(): lax.ppermute(value, axis, [(source, source + steps) for source in range(f...  32.7 us
    ppermute x8, starting transfers between devices, passed_along(): lax.ppermute(value, axis, [(source, source + steps) for source in range(f...  27.1 us
    dot_general x8, matrix products, absorb(): jnp.dot(branch_weights.astype(jnp.bfloat16), some_values, preferred_eleme...  23.5 us
    all_to_all x1, starting transfers between devices, on_device(): lax.all_to_all(sent_keys, 'ctx', split_axis=0, concat_axis=0, tiled=True)  17.3 us
    unnamed x51, local copies, waits for them, and re-layouts  15 us
  transfers between devices with their start and end apart: 13, of which 4 were waited for; matrix products, arithmetic and copies ran while one was open for 40% of the time, Pallas kernels for 0%

commit v1 on v0

--- a/solution.py
+++ b/solution.py
@@ -89,8 +89,13 @@
         jnp.zeros((row_count,), jnp.float32),
         jnp.zeros((row_count, value_width), jnp.float32),
     )
-    piece_keys = lax.all_gather(packed_keys, "ctx", axis=0, tiled=True)
-    piece_values = lax.all_gather(packed_values, "ctx", axis=0, tiled=True)
+    piece_keys, piece_values = jnp.split(
+        lax.all_gather(
+            jnp.concatenate([packed_keys, packed_values], axis=1), "ctx", axis=0, tiled=True
+        ),
+        [packed_keys.shape[1]],
+        axis=1,
+    )
     length = piece_keys.shape[0]
     stride = math.gcd(length, 1024)
     key_block = piece_keys.reshape(length // stride, stride, key_width)

time: 365 us -> 415 us (1.14)
  the two profiles are of different devices: /device:TPU:24 before, /device:TPU:30 now
where the time goes in v1:
time: 415 us; the launch traced here: 413 us
  waiting for transfers between devices  154 us (37%)
  matrix products  81.1 us (20%)
  other arithmetic  57.6 us (14%)
  local copies, waits for them, and re-layouts  49.4 us (12%)
  starting transfers between devices  37.4 us (9%)
  blocking collectives  19.3 us (5%)
  between operations  14 us (3%)
    ppermute x8, waiting for transfers between devices, passed_along(): lax.ppermute(value, axis, [(source, source + steps) for source in range(f...  118 us
    dot_general x8, matrix products, absorb(): lax.dot_general(query_rows, some_keys, (((1,), (1,)), ((), ())), preferre...  44.9 us
    reduce_sum x8, other arithmetic, absorb(): running_total = running_total * factor + jnp.sum(branch_weights, axis=1)  39.5 us
    all_to_all x1, waiting for transfers between devices, on_device(): lax.all_to_all(sent_values, 'ctx', split_axis=0, concat_axis=0, tiled=True)  36 us
    dot_general x8, matrix products, absorb(): jnp.dot(branch_weights.astype(jnp.bfloat16), some_values, preferred_eleme...  23.5 us
    ppermute x8, starting transfers between devices, passed_along(): lax.ppermute(value, axis, [(source, source + steps) for source in range(f...  23 us
    all_to_all x1, blocking collectives, on_device(): lax.all_to_all(asked_here, 'ctx', split_axis=0, concat_axis=0, tiled=True)  19.3 us
    unnamed x44, local copies, waits for them, and re-layouts  17.5 us
  transfers between devices with their start and end apart: 11, of which 5 were waited for; matrix products, arithmetic and copies ran while one was open for 10% of the time, Pallas kernels for 0%

profile of v1, /device:TPU:30, one launch (start us, length us, event | category | flops | bytes accessed | tf_op | source)
XLA Modules:
  0.0 413.2 jit_solution(11003531755327887821)
XLA Ops:
  9.6 19.3 %all_to_all.19 = s32[32,1,4]{2,1,0:T(1,128)S(1)} all-to-all(s32[32,1,4]{2,1,0:T(1,128)S(1)} %bitcast.115), channel_id=1, replica_groups=mesh['ctx'=32,'pb'=2,'ga'=4] {'ctx'}, dimensions={0} | all-to-all | bytes 1024 | tf_op jit(solution)/shard_map/all_to_all | solution.py:136
  32.6 6.6 %all-to-all-start.2 = ((bf16[32,4,64,128]{3,2,1,0:T(8,128)(2,1)}), bf16[32,4,64,128]{3,2,1,0:T(8,128)(2,1)}, u32[]{:S(2)}, u32[]{:S(2)}) async-start(bf16[32,4,64,128]{3,2,1,0:T(8,128)(2,1)} %broadcast_select_fusion.1), calls=%async_computation.2 | async-start | bytes 4194304 | tf_op jit(solution)/shard_map/all_to_all | solution.py:146
  55.3 36.0 %all-to-all-done.2 = bf16[32,4,64,128]{3,2,1,0:T(8,128)(2,1)} async-done(((bf16[32,4,64,128]{3,2,1,0:T(8,128)(2,1)}), bf16[32,4,64,128]{3,2,1,0:T(8,128)(2,1)}, u32[]{:S(2)}, u32[]{:S(2)}) %all-to-all-start.2) | async-done | bytes 2097184 | tf_op jit(solution)/shard_map/all_to_all | solution.py:146
  91.3 7.7 %all-to-all-start.1 = ((bf16[32,4,64,192]{3,2,1,0:T(8,128)(2,1)}), bf16[32,4,64,192]{3,2,1,0:T(8,128)(2,1)}, u32[]{:S(2)}, u32[]{:S(2)}) async-start(bf16[32,4,64,192]{3,2,1,0:T(8,128)(2,1)} %broadcast_select_fusion), calls=%async_computation.1 | async-start | bytes 8388608 | tf_op jit(solution)/shard_map/all_to_all | solution.py:145
  120.6 101.2 %collective-permute-done.4 = bf16[128,128]{0,1:T(8,128)(2,1)S(1)} collective-permute-done((bf16[128,128]{0,1:T(8,128)(2,1)S(1)}, bf16[128,128]{0,1:T(8,128)(2,1)S(1)}, u32[]{:S(2)}, u32[]{:S(2)}) %collective-permute-start.4) | collective-permute-done | bytes 32800 | tf_op jit(solution)/shard_map/ppermute | solution.py:15
  223.7 6.3 %collective-permute-done.5 = bf16[128,128]{0,1:T(8,128)(2,1)S(1)} collective-permute-done((bf16[128,128]{0,1:T(8,128)(2,1)S(1)}, bf16[128,128]{0,1:T(8,128)(2,1)S(1)}, u32[]{:S(2)}, u32[]{:S(2)}) %collective-permute-start.5) | collective-permute-done | bytes 32800 | tf_op jit(solution)/shard_map/ppermute | solution.py:15
  232.6 5.3 %collective-permute-done.6 = bf16[128,128]{0,1:T(8,128)(2,1)S(1)} collective-permute-done((bf16[128,128]{0,1:T(8,128)(2,1)S(1)}, bf16[128,128]{0,1:T(8,128)(2,1)S(1)}, u32[]{:S(2)}, u32[]{:S(2)}) %collective-permute-start.6) | collective-permute-done | bytes 32800 | tf_op jit(solution)/shard_map/ppermute | solution.py:15
  240.1 5.2 %collective-permute-done.7 = bf16[128,128]{0,1:T(8,128)(2,1)S(1)} collective-permute-done((bf16[128,128]{0,1:T(8,128)(2,1)S(1)}, bf16[128,128]{0,1:T(8,128)(2,1)S(1)}, u32[]{:S(2)}, u32[]{:S(2)}) %collective-permute-start.7) | collective-permute-done | bytes 32800 | tf_op jit(solution)/shard_map/ppermute | solution.py:15
  271.2 6.0 %copy.107 = bf16[8192,192]{1,0:T(8,128)(2,1)} copy(bf16[8192,192]{0,1:T(8,128)(2,1)} %split.8) | data formatting | bytes 6291456
  284.3 114.8 %while.15 = (s32[]{:T(128)}, f32[2048]{0:T(1024)S(1)}, f32[2048]{0:T(1024)S(1)}, f32[2048,128]{1,0:T(8,128)S(1)}, bf16[8,1024,192]{2,1,0:T(8,128)(2,1)}, /*index...) while((s32[]{:T(128)}, f32[2048]{0:T(1024)S(1)}, ...), condition=%wide.region_7.8_spmd.clone, body=%wide.region_4.7_spmd.clone.sunk | while | flops 1359751168 | bytes 62522500 | solution.py:122
  284.3 5.6 %multiply_reduce_fusion.2 = (f32[2048]{0:T(1024)S(1)}, f32[1024,2048]{1,0:T(8,128)}) fusion(bf16[2048,192]{1,0:T(8,128)(2,1)S(1)} %get-tuple-element.209, bf16[8,1024,192]{2,1,0:T(8,128)(2,1)} %get-tuple-element.208, s32[]{:T(128)} %get-tuple-element.195), kind=kOutput, calls=%fused_computation.5.clone.1 | convolution fusion | flops 809498624 | bytes 9708032 | tf_op jit(solution)/shard_map/while/body/eval_jaxpr/dot_general | solution.py:108
  289.9 4.9 %fusion.72 = f32[2048]{0:T(1024)S(1)} fusion(f32[1024,2048]{1,0:T(8,128)} %get-tuple-element.183, f32[2048]{0:T(1024)S(1)} %select_maximum_fusion.2), kind=kLoop, calls=%fused_computation.7.clone.1 | loop fusion | flops 6289408 | bytes 8404992 | tf_op jit(solution)/shard_map/while/body/eval_jaxpr/reduce_sum | solution.py:116
  298.7 5.6 %multiply_reduce_fusion.2 = (f32[2048]{0:T(1024)S(1)}, f32[1024,2048]{1,0:T(8,128)}) fusion(bf16[2048,192]{1,0:T(8,128)(2,1)S(1)} %get-tuple-element.209, bf16[8,1024,192]{2,1,0:T(8,128)(2,1)} %get-tuple-element.208, s32[]{:T(128)} %get-tuple-element.195), kind=kOutput, calls=%fused_computation.5.clone.1 | convolution fusion | flops 809498624 | bytes 9708032 | tf_op jit(solution)/shard_map/while/body/eval_jaxpr/dot_general | solution.py:108
  304.3 4.9 %fusion.72 = f32[2048]{0:T(1024)S(1)} fusion(f32[1024,2048]{1,0:T(8,128)} %get-tuple-element.183, f32[2048]{0:T(1024)S(1)} %select_maximum_fusion.2), kind=kLoop, calls=%fused_computation.7.clone.1 | loop fusion | flops 6289408 | bytes 8404992 | tf_op jit(solution)/shard_map/while/body/eval_jaxpr/reduce_sum | solution.py:116
  313.0 5.6 %multiply_reduce_fusion.2 = (f32[2048]{0:T(1024)S(1)}, f32[1024,2048]{1,0:T(8,128)}) fusion(bf16[2048,192]{1,0:T(8,128)(2,1)S(1)} %get-tuple-element.209, bf16[8,1024,192]{2,1,0:T(8,128)(2,1)} %get-tuple-element.208, s32[]{:T(128)} %get-tuple-element.195), kind=kOutput, calls=%fused_computation.5.clone.1 | convolution fusion | flops 809498624 | bytes 9708032 | tf_op jit(solution)/shard_map/while/body/eval_jaxpr/dot_general | solution.py:108
  318.6 4.9 %fusion.72 = f32[2048]{0:T(1024)S(1)} fusion(f32[1024,2048]{1,0:T(8,128)} %get-tuple-element.183, f32[2048]{0:T(1024)S(1)} %select_maximum_fusion.2), kind=kLoop, calls=%fused_computation.7.clone.1 | loop fusion | flops 6289408 | bytes 8404992 | tf_op jit(solution)/shard_map/while/body/eval_jaxpr/reduce_sum | solution.py:116
  327.4 5.6 %multiply_reduce_fusion.2 = (f32[2048]{0:T(1024)S(1)}, f32[1024,2048]{1,0:T(8,128)}) fusion(bf16[2048,192]{1,0:T(8,128)(2,1)S(1)} %get-tuple-element.209, bf16[8,1024,192]{2,1,0:T(8,128)(2,1)} %get-tuple-element.208, s32[]{:T(128)} %get-tuple-element.195), kind=kOutput, calls=%fused_computation.5.clone.1 | convolution fusion | flops 809498624 | bytes 9708032 | tf_op jit(solution)/shard_map/while/body/eval_jaxpr/dot_general | solution.py:108
  333.0 4.9 %fusion.72 = f32[2048]{0:T(1024)S(1)} fusion(f32[1024,2048]{1,0:T(8,128)} %get-tuple-element.183, f32[2048]{0:T(1024)S(1)} %select_maximum_fusion.2), kind=kLoop, calls=%fused_computation.7.clone.1 | loop fusion | flops 6289408 | bytes 8404992 | tf_op jit(solution)/shard_map/while/body/eval_jaxpr/reduce_sum | solution.py:116
  341.7 5.6 %multiply_reduce_fusion.2 = (f32[2048]{0:T(1024)S(1)}, f32[1024,2048]{1,0:T(8,128)}) fusion(bf16[2048,192]{1,0:T(8,128)(2,1)S(1)} %get-tuple-element.209, bf16[8,1024,192]{2,1,0:T(8,128)(2,1)} %get-tuple-element.208, s32[]{:T(128)} %get-tuple-element.195), kind=kOutput, calls=%fused_computation.5.clone.1 | convolution fusion | flops 809498624 | bytes 9708032 | tf_op jit(solution)/shard_map/while/body/eval_jaxpr/dot_general | solution.py:108
  347.3 4.9 %fusion.72 = f32[2048]{0:T(1024)S(1)} fusion(f32[1024,2048]{1,0:T(8,128)} %get-tuple-element.183, f32[2048]{0:T(1024)S(1)} %select_maximum_fusion.2), kind=kLoop, calls=%fused_computation.7.clone.1 | loop fusion | flops 6289408 | bytes 8404992 | tf_op jit(solution)/shard_map/while/body/eval_jaxpr/reduce_sum | solution.py:116
  356.1 5.6 %multiply_reduce_fusion.2 = (f32[2048]{0:T(1024)S(1)}, f32[1024,2048]{1,0:T(8,128)}) fusion(bf16[2048,192]{1,0:T(8,128)(2,1)S(1)} %get-tuple-element.209, bf16[8,1024,192]{2,1,0:T(8,128)(2,1)} %get-tuple-element.208, s32[]{:T(128)} %get-tuple-element.195), kind=kOutput, calls=%fused_computation.5.clone.1 | convolution fusion | flops 809498624 | bytes 9708032 | tf_op jit(solution)/shard_map/while/body/eval_jaxpr/dot_general | solution.py:108
  361.7 4.9 %fusion.72 = f32[2048]{0:T(1024)S(1)} fusion(f32[1024,2048]{1,0:T(8,128)} %get-tuple-element.183, f32[2048]{0:T(1024)S(1)} %select_maximum_fusion.2), kind=kLoop, calls=%fused_computation.7.clone.1 | loop fusion | flops 6289408 | bytes 8404992 | tf_op jit(solution)/shard_map/while/body/eval_jaxpr/reduce_sum | solution.py:116
  370.4 5.6 %multiply_reduce_fusion.2 = (f32[2048]{0:T(1024)S(1)}, f32[1024,2048]{1,0:T(8,128)}) fusion(bf16[2048,192]{1,0:T(8,128)(2,1)S(1)} %get-tuple-element.209, bf16[8,1024,192]{2,1,0:T(8,128)(2,1)} %get-tuple-element.208, s32[]{:T(128)} %get-tuple-element.195), kind=kOutput, calls=%fused_computation.5.clone.1 | convolution fusion | flops 809498624 | bytes 9708032 | tf_op jit(solution)/shard_map/while/body/eval_jaxpr/dot_general | solution.py:108
  384.8 5.6 %multiply_reduce_fusion.2 = (f32[2048]{0:T(1024)S(1)}, f32[1024,2048]{1,0:T(8,128)}) fusion(bf16[2048,192]{1,0:T(8,128)(2,1)S(1)} %get-tuple-element.209, bf16[8,1024,192]{2,1,0:T(8,128)(2,1)} %get-tuple-element.208, s32[]{:T(128)} %get-tuple-element.195), kind=kOutput, calls=%fused_computation.5.clone.1 | convolution fusion | flops 809498624 | bytes 9708032 | tf_op jit(solution)/shard_map/while/body/eval_jaxpr/dot_general | solution.py:108
  (180 shorter events, 130.8 us)
Async XLA Ops:
  6.5 23.4 %copy-start = (bf16[4096,128]{1,0:T(8,128)(2,1)S(1)}, bf16[4096,128]{1,0:T(8,128)(2,1)}, u32[]{:S(2)}) copy-start(bf16[4096,128]{1,0:T(8,128)(2,1)} %param.16) | copy-start | bytes 3145732
  30.9 8.3 %copy-start.12 = (s32[1,256]{1,0:T(1,128)S(1)}, s32[1,256]{1,0:T(1,128)}, u32[]{:S(2)}) copy-start(s32[1,256]{1,0:T(1,128)} %param.17) | copy-start | bytes 3076
  30.9 10.3 %copy-start.14 = (f32[1,32]{1,0:T(1,128)S(1)}, f32[1,32]{1,0:T(1,128)}, u32[]{:S(2)}) copy-start(f32[1,32]{1,0:T(1,128)} %param.18) | copy-start | bytes 388
  32.6 58.7 %all-to-all-start.2 = ((bf16[32,4,64,128]{3,2,1,0:T(8,128)(2,1)}), bf16[32,4,64,128]{3,2,1,0:T(8,128)(2,1)}, u32[]{:S(2)}, u32[]{:S(2)}) async-start(bf16[32,4,64,128]{3,2,1,0:T(8,128)(2,1)} %broadcast_select_fusion.1), calls=%async_computation.2 | async-start | bytes 4194304 | tf_op jit(solution)/shard_map/all_to_all | solution.py:146
  39.2 228.2 %all-gather.2.cloned.1.call-start = ((), (), s32[]{:S(2)}) async-start(), calls=%async_computation.3 | async-start | bytes 5406720 | tf_op jit(solution)/shard_map/all_gather | solution.py:93
  55.2 43.8 %copy-start.9 = (bf16[128,192]{0,1:T(8,128)(2,1)S(1)}, bf16[128,192]{0,1:T(8,128)(2,1)}, u32[]{:S(2)}) copy-start(bf16[128,192]{0,1:T(8,128)(2,1)} %param.13) | copy-start | bytes 147460
  55.2 57.8 %copy-start.10 = (bf16[128,128]{1,0:T(8,128)(2,1)S(1)}, bf16[128,128]{1,0:T(8,128)(2,1)}, u32[]{:S(2)}) copy-start(bf16[128,128]{1,0:T(8,128)(2,1)} %param.14) | copy-start | bytes 98308
  55.2 60.4 %copy-start.13 = (s32[2,1,13]{2,1,0:T(1,128)S(1)}, s32[2,1,13]{2,1,0:T(1,128)}, u32[]{:S(2)}) copy-start(s32[2,1,13]{2,1,0:T(1,128)} %param.19) | copy-start | bytes 316
  55.2 60.6 %copy-start.15 = (s32[3,1]{0,1:T(1,128)S(1)}, s32[3,1]{0,1:T(1,128)}, u32[]{:S(2)}) copy-start(s32[3,1]{0,1:T(1,128)} %constant.143) | copy-start | bytes 40
  55.2 60.6 %copy-start.11 = (f32[3,128,16]{1,2,0:T(8,128)S(1)}, f32[3,128,16]{1,2,0:T(8,128)}, u32[]{:S(2)}) copy-start(f32[3,128,16]{1,2,0:T(8,128)} %param.20) | copy-start | bytes 73732
  55.2 60.9 %copy-start.3 = (bf16[128,3072]{1,0:T(8,128)(2,1)S(1)}, bf16[128,3072]{1,0:T(8,128)(2,1)}, u32[]{:S(2)}) copy-start(bf16[128,3072]{1,0:T(8,128)(2,1)} %param.12) | copy-start | bytes 2359300
  91.3 162.9 %all-to-all-start.1 = ((bf16[32,4,64,192]{3,2,1,0:T(8,128)(2,1)}), bf16[32,4,64,192]{3,2,1,0:T(8,128)(2,1)}, u32[]{:S(2)}, u32[]{:S(2)}) async-start(bf16[32,4,64,192]{3,2,1,0:T(8,128)(2,1)} %broadcast_select_fusion), calls=%async_computation.1 | async-start | bytes 8388608 | tf_op jit(solution)/shard_map/all_to_all | solution.py:145
  99.0 146.3 %collective-permute-start = (bf16[128,192]{0,1:T(8,128)(2,1)S(1)}, bf16[128,192]{0,1:T(8,128)(2,1)S(1)}, u32[]{:S(2)}, u32[]{:S(2)}) collective-permute-start(bf16[128,192]{0,1:T(8,128)(2,1)S(1)} %copy-done.9), channel_id=1, source_target_pairs={{0,16},{4,20},{8,24},{12,28},{16,32},{20,36},{24,40},{28,44},{32,4... | collective-permute-start | bytes 147464 | tf_op jit(solution)/shard_map/ppermute | solution.py:15
  103.3 142.0 %collective-permute-start.1 = (bf16[128,192]{0,1:T(8,128)(2,1)S(1)}, bf16[128,192]{0,1:T(8,128)(2,1)S(1)}, u32[]{:S(2)}, u32[]{:S(2)}) collective-permute-start(bf16[128,192]{0,1:T(8,128)(2,1)S(1)} %copy-done.9), channel_id=1, source_target_pairs={{0,12},{4,16},{8,20},{12,24},{16,28},{20,32},{24,36},{28,40},{32,4... | collective-permute-start | bytes 147464 | tf_op jit(solution)/shard_map/ppermute | solution.py:15
  105.2 140.1 %collective-permute-start.2 = (bf16[128,192]{0,1:T(8,128)(2,1)S(1)}, bf16[128,192]{0,1:T(8,128)(2,1)S(1)}, u32[]{:S(2)}, u32[]{:S(2)}) collective-permute-start(bf16[128,192]{0,1:T(8,128)(2,1)S(1)} %copy-done.9), channel_id=1, source_target_pairs={{0,8},{4,12},{8,16},{12,20},{16,24},{20,28},{24,32},{28,36},{32,40... | collective-permute-start | bytes 147464 | tf_op jit(solution)/shard_map/ppermute | solution.py:15
  108.6 136.8 %collective-permute-start.3 = (bf16[128,192]{0,1:T(8,128)(2,1)S(1)}, bf16[128,192]{0,1:T(8,128)(2,1)S(1)}, u32[]{:S(2)}, u32[]{:S(2)}) collective-permute-start(bf16[128,192]{0,1:T(8,128)(2,1)S(1)} %copy-done.9), channel_id=1, source_target_pairs={{0,4},{4,8},{8,12},{12,16},{16,20},{20,24},{24,28},{28,32},{32,36}... | collective-permute-start | bytes 147464 | tf_op jit(solution)/shard_map/ppermute | solution.py:15
  113.2 108.6 %collective-permute-start.4 = (bf16[128,128]{0,1:T(8,128)(2,1)S(1)}, bf16[128,128]{0,1:T(8,128)(2,1)S(1)}, u32[]{:S(2)}, u32[]{:S(2)}) collective-permute-start(bf16[128,128]{0,1:T(8,128)(2,1)S(1)} %copy.97), channel_id=1, source_target_pairs={{0,16},{4,20},{8,24},{12,28},{16,32},{20,36},{24,40},{28,44},{32,4... | collective-permute-start | bytes 98312 | tf_op jit(solution)/shard_map/ppermute | solution.py:15
  221.8 8.2 %collective-permute-start.5 = (bf16[128,128]{0,1:T(8,128)(2,1)S(1)}, bf16[128,128]{0,1:T(8,128)(2,1)S(1)}, u32[]{:S(2)}, u32[]{:S(2)}) collective-permute-start(bf16[128,128]{0,1:T(8,128)(2,1)S(1)} %copy.97), channel_id=1, source_target_pairs={{0,12},{4,16},{8,20},{12,24},{16,28},{20,32},{24,36},{28,40},{32,4... | collective-permute-start | bytes 98312 | tf_op jit(solution)/shard_map/ppermute | solution.py:15
  230.0 7.9 %collective-permute-start.6 = (bf16[128,128]{0,1:T(8,128)(2,1)S(1)}, bf16[128,128]{0,1:T(8,128)(2,1)S(1)}, u32[]{:S(2)}, u32[]{:S(2)}) collective-permute-start(bf16[128,128]{0,1:T(8,128)(2,1)S(1)} %copy.97), channel_id=1, source_target_pairs={{0,8},{4,12},{8,16},{12,20},{16,24},{20,28},{24,32},{28,36},{32,40... | collective-permute-start | bytes 98312 | tf_op jit(solution)/shard_map/ppermute | solution.py:15
  237.9 7.3 %collective-permute-start.7 = (bf16[128,128]{0,1:T(8,128)(2,1)S(1)}, bf16[128,128]{0,1:T(8,128)(2,1)S(1)}, u32[]{:S(2)}, u32[]{:S(2)}) collective-permute-start(bf16[128,128]{0,1:T(8,128)(2,1)S(1)} %copy.97), channel_id=1, source_target_pairs={{0,4},{4,8},{8,12},{12,16},{16,20},{20,24},{24,28},{28,32},{32,36}... | collective-permute-start | bytes 98312 | tf_op jit(solution)/shard_map/ppermute | solution.py:15
  289.9 5.8 %copy-start.2 = (f32[1024,2048]{1,0:T(8,128)S(1)}, f32[1024,2048]{1,0:T(8,128)}, u32[]{:S(2)}) copy-start(f32[1024,2048]{1,0:T(8,128)} %get-tuple-element.183) | copy-start | bytes 25165828 | tf_op jit(solution)/shard_map/while
  318.6 5.8 %copy-start.2 = (f32[1024,2048]{1,0:T(8,128)S(1)}, f32[1024,2048]{1,0:T(8,128)}, u32[]{:S(2)}) copy-start(f32[1024,2048]{1,0:T(8,128)} %get-tuple-element.183) | copy-start | bytes 25165828 | tf_op jit(solution)/shard_map/while
  333.0 5.8 %copy-start.2 = (f32[1024,2048]{1,0:T(8,128)S(1)}, f32[1024,2048]{1,0:T(8,128)}, u32[]{:S(2)}) copy-start(f32[1024,2048]{1,0:T(8,128)} %get-tuple-element.183) | copy-start | bytes 25165828 | tf_op jit(solution)/shard_map/while
  361.7 5.8 %copy-start.2 = (f32[1024,2048]{1,0:T(8,128)S(1)}, f32[1024,2048]{1,0:T(8,128)}, u32[]{:S(2)}) copy-start(f32[1024,2048]{1,0:T(8,128)} %get-tuple-element.183) | copy-start | bytes 25165828 | tf_op jit(solution)/shard_map/while
  (10 other events, 43.6 us)
Sparse Core Ops, SparseCore 0:
  44.8 168.7 all-gather.1
